TPU v7x, 32 devices: a whole 2x2x4 slice. The times are simulated.
32 devices in a mesh: dp: 8 (over y, x, core), pencil: 4 (over z).
Axes of the slice: x: 2, y: 2, z: 4, core: 2. Of those that a mesh axis runs over, the one named last changes fastest.
Arguments:
- field: bfloat16 [8, 64, 64, 64, 128], P('dp', 'pencil'), may hold values from -6 to 6
- cotangent: bfloat16 [8, 64, 64, 64, 128], P('dp', 'pencil'), may hold values from -6 to 6
- w_spec: bfloat16 [16, 16, 16, 64, 128], P('dp', 'pencil'), may hold values from -6 to 6
- w_local: bfloat16 [64, 64], replicated, may hold values from -0.75 to 0.75
Outputs:
- grad_field: bfloat16 [8, 64, 64, 64, 128], P('dp', 'pencil')
- grad_w: float32 [16, 16, 16, 64, 128], P('dp', 'pencil')
All inputs are finite; a program needn't handle non-finite values.
Results may differ from a plain program's by a relative error of at most 0.02.
Values may be sent and summed in bfloat16 or wider, within the bound.
A program may use at most 192 MiB of HBM per device.

v0:
```python
import functools
import math

import jax
import jax.numpy as jnp
import numpy as np
from jax import lax
from jax.experimental import pallas as pl
from jax.experimental.pallas import tpu as pltpu
from jax.sharding import PartitionSpec as P

BF16 = jnp.bfloat16
F32 = jnp.float32
ROWS = 16
NXB = 2
YB = 4
VMEM = 64 * 1000 * 1024


def waves(length, count, signed):
    index = np.arange(count)
    freq = np.where(index < count // 2, index, index - count) if signed else index
    angle = 2.0 * math.pi * ((np.arange(length)[:, None] * freq[None, :]) % length) / length
    return np.cos(angle), np.sin(angle)


def kron_rows(matrix):
    return np.kron(matrix, np.eye(ROWS))


def const(array):
    return jnp.asarray(np.asarray(array, np.float32), BF16)


def make_tables(nx, ny, nz, groups, mx, my, mz, pencils):
    cx, sx = waves(nx, mx, True)
    cy, sy = waves(ny, my, True)
    cz, sz = waves(nz, mz, False)
    eye_g = np.eye(groups)
    plain = np.concatenate([cz, -sz], 1)
    turned = np.concatenate([-sz, -cz], 1)
    z_fwd = np.concatenate([np.kron(eye_g, plain), np.kron(eye_g, turned)], 1)
    weight = np.where(np.arange(mz) == 0, 1.0, 2.0) / (nx * ny * nz)
    z_inv = np.kron(eye_g, np.concatenate([cz * weight, -sz * weight], 1).T)
    z_adj = np.kron(eye_g, plain.T)
    half = np.eye(mz)
    zero = np.zeros((mz, mz))
    turn = np.kron(eye_g, np.block([[zero, -half], [half, zero]]))
    y_fwd = np.concatenate([kron_rows(cy.T), kron_rows(sy.T)], 1)
    y_inv = np.concatenate([kron_rows(cy), -kron_rows(sy)], 1)
    own = nx // pencils
    x_fwd, x_inv = [], []
    for q in range(pencils):
        c, s = cx[q * own : (q + 1) * own], sx[q * own : (q + 1) * own]
        x_fwd.append(np.concatenate([kron_rows(c.T), kron_rows(s.T)], 1))
        x_inv.append(np.concatenate([kron_rows(c), -kron_rows(s)], 1))
    scale = np.tile(np.concatenate([weight, weight]), groups)
    return dict(
        z_fwd=const(z_fwd),
        z_inv=const(z_inv),
        z_adj=const(z_adj),
        turn=const(turn),
        y_fwd=const(y_fwd),
        y_inv=const(y_inv),
        x_fwd=const(np.stack(x_fwd)),
        x_inv=const(np.stack(x_inv)),
        scale=jnp.asarray(scale, F32),
    )


def mm(a, b):
    return jnp.dot(a, b, preferred_element_type=F32)


def forward_zy(src, z_fwd, y_fwd, sections, step):
    nxb, ny, ch, nz = src.shape
    groups = ch // ROWS
    lanes = z_fwd.shape[1] // 2
    plain, turned = [], []
    for x in range(nxb):
        wide = jnp.concatenate(
            [src[x, :, g * ROWS : (g + 1) * ROWS, :].reshape(ny * ROWS, nz) for g in range(groups)], 1
        )
        spectral = mm(wide, z_fwd[...]).astype(BF16)
        plain.append(spectral[:, :lanes])
        turned.append(spectral[:, lanes:])
    stacked = jnp.concatenate([jnp.concatenate(plain, 1), jnp.concatenate(turned, 1)], 0)
    out = mm(y_fwd[...], stacked).astype(BF16)
    for x in range(nxb):
        sections[step * nxb + x] = out[:, x * lanes : (x + 1) * lanes]


def forward_x(sections, x_fwd, turn, out):
    pd, pp, jxl, jyl, _, lanes = out.shape
    xl = sections.shape[0]
    for p in range(pp):
        for b in range(jyl):
            j = p * jyl + b
            rows = sections[:, j * ROWS : (j + 1) * ROWS, :].reshape(xl * ROWS, lanes)
            both = jnp.concatenate([rows, mm(rows, turn[...]).astype(BF16)], 0)
            got = mm(x_fwd[...], both).astype(BF16)
            out[:, p, :, b] = got.reshape(pd, jxl, ROWS, lanes)


def inverse_x(modes, x_inv, turn, sections):
    pd, pp, jxl, jyl, _, lanes = modes.shape
    xl = sections.shape[0]
    for p in range(pp):
        for b in range(jyl):
            j = p * jyl + b
            rows = modes[:, p, :, b].reshape(pd * jxl * ROWS, lanes)
            both = jnp.concatenate([rows, mm(rows, turn[...]).astype(BF16)], 0)
            got = mm(x_inv[...], both).astype(BF16)
            sections[:, j * ROWS : (j + 1) * ROWS, :] = got.reshape(xl, ROWS, lanes)


def inverse_y(sections, turn, y_inv, columns, step, nxb):
    plain = [sections[step * nxb + x] for x in range(nxb)]
    turned = [mm(v, turn[...]).astype(BF16) for v in plain]
    stacked = jnp.concatenate([jnp.concatenate(plain, 1), jnp.concatenate(turned, 1)], 0)
    columns[...] = mm(y_inv[...], stacked).astype(BF16)


def inverse_z_mix(columns, z_inv, mix, src, emit):
    nxb, ny, ch, nz = src.shape
    groups = ch // ROWS
    lanes = z_inv.shape[0]

    def block(i, carry):
        y0 = pl.multiple_of(i * YB, YB)
        cols = columns[pl.ds(pl.multiple_of(i * (YB * ROWS), YB * ROWS), YB * ROWS), :]
        wide = jnp.concatenate([src[x, pl.ds(y0, YB)].reshape(YB * ch, nz) for x in range(nxb)], 1)
        mixed = mm(mix[...], wide)
        for x in range(nxb):
            grid = mm(cols[:, x * lanes : (x + 1) * lanes], z_inv[...]).reshape(YB, ROWS, groups * nz)
            grid = jnp.concatenate([grid[:, :, g * nz : (g + 1) * nz] for g in range(groups)], 1)
            emit(x, y0, grid + mixed[:, x * nz : (x + 1) * nz].reshape(YB, ch, nz))
        return carry

    lax.fori_loop(0, ny // YB, block, 0, unroll=2)


def gelu_slope(pre):
    normal_cdf = 0.5 * (1.0 + lax.erf(pre * (1.0 / math.sqrt(2.0))))
    return normal_cdf + pre * jnp.exp(-0.5 * pre * pre) * (1.0 / math.sqrt(2.0 * math.pi))


def first_kernel(field, z_fwd, y_fwd, x_fwd, turn, out, sections):
    step = pl.program_id(0)
    forward_zy(field, z_fwd, y_fwd, sections, step)

    @pl.when(step == pl.num_programs(0) - 1)
    def _():
        forward_x(sections, x_fwd, turn, out)


def middle_kernel(
    modes, field, target, mix, z_inv, y_inv, x_inv, z_fwd, y_fwd, x_fwd, turn,
    slope, out, sections_in, columns, sections_out,
):
    step = pl.program_id(0)

    @pl.when(step == 0)
    def _():
        inverse_x(modes, x_inv, turn, sections_in)

    inverse_y(sections_in, turn, y_inv, columns, step, field.shape[0])

    def emit(x, y0, pre):
        cot = target[x, pl.ds(y0, YB)].astype(F32)
        slope[x, pl.ds(y0, YB)] = (cot * gelu_slope(pre)).astype(BF16)

    inverse_z_mix(columns, z_inv, mix, field, emit)
    forward_zy(slope, z_fwd, y_fwd, sections_out, step)

    @pl.when(step == pl.num_programs(0) - 1)
    def _():
        forward_x(sections_out, x_fwd, turn, out)


def last_kernel(modes, slope, mix, z_adj, y_inv, x_inv, turn, grad, sections, columns):
    step = pl.program_id(0)

    @pl.when(step == 0)
    def _():
        inverse_x(modes, x_inv, turn, sections)

    inverse_y(sections, turn, y_inv, columns, step, slope.shape[0])

    def emit(x, y0, value):
        grad[x, pl.ds(y0, YB)] = value.astype(BF16)

    inverse_z_mix(columns, z_adj, mix, slope, emit)


def whole(array):
    return pl.BlockSpec(array.shape, lambda i, n=len(array.shape): (0,) * n)


def sliced(shape):
    return pl.BlockSpec((NXB,) + shape[1:], lambda i: (i, 0, 0, 0))


def params():
    return pltpu.CompilerParams(dimension_semantics=("arbitrary",), vmem_limit_bytes=VMEM)


def load_modes(parts, scale, by_mode):
    pd, pp, _, rows, lanes = parts.shape
    total = parts[:, 0, 0].astype(F32)
    for q in range(1, pp):
        total = total + parts[:, q, 0].astype(F32)
    total = total * scale[...]
    turned = total.reshape(pd * rows, lanes).T
    count = by_mode.shape[0]
    for s in range(pd):
        own = turned[:, s * rows : (s + 1) * rows]
        pieces = [own[g * count : (g + 1) * count] for g in range(lanes // count)]
        by_mode[:, s, :] = jnp.concatenate(pieces, 1)


def store_modes(by_mode, out):
    pd, pp, _, rows, lanes = out.shape
    count = by_mode.shape[0]
    columns = []
    for s in range(pd):
        own = by_mode[:, s, :]
        pieces = [own[:, g * rows : (g + 1) * rows] for g in range(lanes // count)]
        columns.append(jnp.concatenate(pieces, 0))
    turned = jnp.concatenate(columns, 1).T.reshape(pd, rows, lanes).astype(BF16)
    for q in range(pp):
        out[:, q, 0] = turned


def apply_kernel(parts, w, scale, u, out, by_mode, result):
    load_modes(parts, scale, by_mode)
    mz, ch = w.shape[0], w.shape[1]
    half = by_mode.shape[1]
    for k in range(mz):
        uk = jnp.concatenate([by_mode[k], by_mode[mz + k]], 0).astype(BF16)
        u[k] = uk
        d = mm(uk, w[k])
        result[k] = d[:half, :ch] - d[half:, ch:]
        result[mz + k] = d[:half, ch:] + d[half:, :ch]
    store_modes(result, out)


def adjoint_kernel(parts, w, scale, u, grad_w, out, by_mode, result):
    load_modes(parts, scale, by_mode)
    mz = w.shape[0]
    half = by_mode.shape[1]
    for k in range(mz):
        real, imag = by_mode[k], by_mode[mz + k]
        pair = jnp.concatenate(
            [jnp.concatenate([real, imag], 1), jnp.concatenate([imag, -real], 1)], 0
        ).astype(BF16)
        back = lax.dot_general(pair, w[k], (((1,), (1,)), ((), ())), preferred_element_type=F32)
        result[k] = back[:half]
        result[mz + k] = back[half:]
        grad_w[k] = lax.dot_general(
            u[k], pair, (((0,), (0,)), ((), ())), preferred_element_type=F32
        )
    store_modes(result, out)


def mode_call(kernel, parts, w, scale, u):
    pd, pp, count, rows, lanes = parts.shape
    mz, ch = w.shape[0] // count, w.shape[1]
    first = u is None
    part_spec = pl.BlockSpec((pd, pp, 1, rows, lanes), lambda i: (0, 0, i, 0, 0))
    w_spec = pl.BlockSpec((mz,) + w.shape[1:], lambda i: (i, 0, 0))
    u_spec = pl.BlockSpec((mz, 2 * pd, ch), lambda i: (i, 0, 0))
    u_shape = jax.ShapeDtypeStruct((w.shape[0], 2 * pd, ch), BF16)
    w_shape = jax.ShapeDtypeStruct(w.shape, F32)
    by_mode = pltpu.VMEM((2 * mz, pd, ch), F32)
    return pl.pallas_call(
        kernel,
        grid=(count,),
        in_specs=[part_spec, w_spec, whole(scale)] + ([] if first else [u_spec]),
        out_specs=[u_spec if first else w_spec, part_spec],
        out_shape=[u_shape if first else w_shape, jax.ShapeDtypeStruct(parts.shape, BF16)],
        scratch_shapes=[by_mode, by_mode],
        compiler_params=params(),
    )(parts, w, scale, *(() if first else (u,)))


def solution(mesh):
    pd, pp = mesh.shape["dp"], mesh.shape["pencil"]
    axes = ("dp", "pencil")

    def body(field, cotangent, w_spec, w_local):
        sample, target = field[0], cotangent[0]
        xl, ny, ch, nz = sample.shape
        jxl, jyl, mz = w_spec.shape[:3]
        mx, my = jxl * pd, jyl * pp
        groups = ch // ROWS
        lanes = groups * 2 * mz
        t = make_tables(xl * pp, ny, nz, groups, mx, my, mz, pp)
        me = lax.axis_index("pencil")
        x_fwd = lax.dynamic_index_in_dim(t["x_fwd"], me, 0, keepdims=False)
        x_inv = lax.dynamic_index_in_dim(t["x_inv"], me, 0, keepdims=False)
        mix_eye = jnp.eye(YB, dtype=BF16)
        mix_in = jnp.kron(mix_eye, w_local.T)
        mix_out = jnp.kron(mix_eye, w_local)
        sent = jax.ShapeDtypeStruct((pd, pp, jxl, jyl, ROWS, lanes), BF16)
        grid_like = jax.ShapeDtypeStruct(sample.shape, BF16)
        sections = pltpu.VMEM((xl, my * ROWS, lanes), BF16)
        columns = pltpu.VMEM((ny * ROWS, NXB * lanes), BF16)
        steps = (xl // NXB,)

        def exchange(array):
            flat = array.reshape((pd * pp,) + array.shape[2:])
            got = lax.all_to_all(flat, axes, split_axis=0, concat_axis=0, tiled=True)
            return got.reshape(array.shape)

        def to_owner(parts):
            return exchange(parts).reshape((pd, pp, jxl * jyl, ROWS, lanes))

        def to_sample(modes):
            return exchange(modes).reshape(sent.shape)

        weights = w_spec.reshape(jxl * jyl * mz, ch, 2 * ch)
        ins = (sample, t["z_fwd"], t["y_fwd"], x_fwd, t["turn"])
        u_parts = pl.pallas_call(
            first_kernel,
            grid=steps,
            in_specs=[sliced(sample.shape)] + [whole(a) for a in ins[1:]],
            out_specs=whole(sent),
            out_shape=sent,
            scratch_shapes=[sections],
            compiler_params=params(),
        )(*ins)
        scale = t["scale"].reshape(1, 1, lanes)
        u_modes, v_modes = mode_call(
            apply_kernel, to_owner(u_parts), weights, jnp.ones_like(scale), None
        )
        ins = (
            to_sample(v_modes), sample, target, mix_in, t["z_inv"], t["y_inv"], x_inv,
            t["z_fwd"], t["y_fwd"], x_fwd, t["turn"],
        )
        slope, g_parts = pl.pallas_call(
            middle_kernel,
            grid=steps,
            in_specs=[whole(ins[0]), sliced(sample.shape), sliced(sample.shape)]
            + [whole(a) for a in ins[3:]],
            out_specs=[sliced(sample.shape), whole(sent)],
            out_shape=[grid_like, sent],
            scratch_shapes=[sections, columns, sections],
            compiler_params=params(),
        )(*ins)
        grad_w, back = mode_call(adjoint_kernel, to_owner(g_parts), weights, scale, u_modes)
        ins = (to_sample(back), slope, mix_out, t["z_adj"], t["y_inv"], x_inv, t["turn"])
        grad = pl.pallas_call(
            last_kernel,
            grid=steps,
            in_specs=[whole(ins[0]), sliced(sample.shape)] + [whole(a) for a in ins[2:]],
            out_specs=sliced(sample.shape),
            out_shape=grid_like,
            scratch_shapes=[sections, columns],
            compiler_params=params(),
        )(*ins)
        return grad[None], grad_w.reshape(w_spec.shape)

    grid_spec = P("dp", "pencil", None, None, None)
    return jax.shard_map(
        body,
        mesh=mesh,
        in_specs=(grid_spec, grid_spec, grid_spec, P()),
        out_specs=(grid_spec, grid_spec),
        check_vma=False,
    )
```

profile of v0, /device:TPU:0, one launch (start us, length us, event | category | flops | bytes accessed | tf_op | source)
XLA Modules:
  0.0 245.2 jit_solution(13620893927349603949)
XLA Ops:
  0.6 0.0 copy-start.2
  0.6 1.7 dynamic-slice_bitcast_fusion.1.x_fwd
  2.3 17.5 %shard_map.140 = bf16[8,4,2,4,16,128]{5,4,3,2,1,0:T(8,128)(2,1)} custom-call(bf16[16,64,64,128]{3,2,1,0:T(8,128)(2,1)} %bitcast.18, bf16[512,256]{1,0:T(8,128)(2,1)} %constant.32.clone.z_fwd, bf16[256,2048]{1,0:T(8,128)(2,1)} %constant.36.clone.y_fwd, bf16[256,512]{1,0:T(8,128)(2,1)} %dynamic-slice_bitcast_fusion.1.x_fwd, bf16[128,128]{1,0:T(8,128)(2,1)} %constant.35.clone.turn), custom_call_target="tpu_custom_call" | custom-call | tf_op jit(solution)/shard_map/pallas_call | solution.py:324
  19.8 32.4 %all_to_all.20 = bf16[32,2,4,16,128]{4,3,2,1,0:T(8,128)(2,1)} all-to-all(bf16[32,2,4,16,128]{4,3,2,1,0:T(8,128)(2,1)} %bitcast.26), channel_id=1, replica_groups=mesh['dp'=8,'pencil'=4] {'dp','pencil'}, dimensions={0} | all-to-all | bytes 2097152 | tf_op jit(solution)/shard_map/all_to_all | solution.py:313
  52.2 0.5 broadcast_in_dim.12.scale
  52.7 9.5 %shard_map.141 = (bf16[128,16,64]{2,1,0:T(8,128)(2,1)}, bf16[8,4,8,16,128]{4,3,2,1,0:T(8,128)(2,1)}) custom-call(bf16[8,4,8,16,128]{4,3,2,1,0:T(8,128)(2,1)} %bitcast.27, bf16[128,64,128]{2,1,0:T(8,128)(2,1)} %bitcast.22, f32[1,1,128]{2,1,0:T(1,128)} %broadcast_in_dim.12.scale), custom_call_target="tpu_custom_call" | custom-call | tf_op jit(solution)/shard_map/pallas_call | solution.py:276
  62.2 4.6 %all-to-all-start.1 = ((bf16[32,8,16,128]{3,2,1,0:T(8,128)(2,1)}), bf16[32,8,16,128]{3,2,1,0:T(8,128)(2,1)S(1)}, u32[]{:S(2)}, u32[]{:S(2)}) async-start(bf16[32,8,16,128]{3,2,1,0:T(8,128)(2,1)} %bitcast.29), calls=%async_computation.1 | async-start | bytes 2097152 | tf_op jit(solution)/shard_map/all_to_all | solution.py:313
  66.8 0.0 copy-done.2
  66.8 0.1 copy.15
  66.9 0.3 broadcast_multiply_fusion
  67.2 0.9 mul.44.mix
  68.0 1.7 dynamic-slice_bitcast_fusion.x_inv
  69.7 22.0 %all-to-all-done.1 = bf16[32,8,16,128]{3,2,1,0:T(8,128)(2,1)S(1)} async-done(((bf16[32,8,16,128]{3,2,1,0:T(8,128)(2,1)}), bf16[32,8,16,128]{3,2,1,0:T(8,128)(2,1)S(1)}, u32[]{:S(2)}, u32[]{:S(2)}) %all-to-all-start.1) | async-done | bytes 1048608 | tf_op jit(solution)/shard_map/all_to_all | solution.py:313
  91.7 0.0 copy-start
  91.7 1.0 copy-done
  92.7 53.0 %shard_map.142 = (bf16[16,64,64,128]{3,2,1,0:T(8,128)(2,1)}, bf16[8,4,2,4,16,128]{5,4,3,2,1,0:T(8,128)(2,1)}) custom-call(bf16[8,4,2,4,16,128]{5,4,3,2,1,0:T(8,128)(2,1)} %bitcast.24, bf16[16,64,64,128]{3,2,1,0:T(8,128)(2,1)} %bitcast.19, bf16[16,64,64,128]{3,2,1,0:T(8,128)(2,1)} %bitcast.21, bf16[256,256]{1,0:T(8,128)(2,1)} %mul.44.mix, ...), custom_call_target="tpu_custom_call" | custom-call | tf_op jit(solution)/shard_map/pallas_call | solution.py:341
  145.6 29.6 %all_to_all.21 = bf16[32,2,4,16,128]{4,3,2,1,0:T(8,128)(2,1)} all-to-all(bf16[32,2,4,16,128]{4,3,2,1,0:T(8,128)(2,1)} %bitcast.31), channel_id=1, replica_groups=mesh['dp'=8,'pencil'=4] {'dp','pencil'}, dimensions={0} | all-to-all | bytes 2097152 | tf_op jit(solution)/shard_map/all_to_all | solution.py:313
  175.2 9.8 %shard_map.143 = (f32[128,64,128]{2,1,0:T(8,128)}, bf16[8,4,8,16,128]{4,3,2,1,0:T(8,128)(2,1)}) custom-call(bf16[8,4,8,16,128]{4,3,2,1,0:T(8,128)(2,1)} %bitcast.28, bf16[128,64,128]{2,1,0:T(8,128)(2,1)} %bitcast.23, f32[1,1,128]{2,1,0:T(1,128)} %constant.44.scale, bf16[128,16,64]{2,1,0:T(8,128)(2,1)} %get-tuple-element.10.u), custom_call_target="tpu_custom_call" | custom-call | tf_op jit(solution)/shard_map/pallas_call | solution.py:276
  185.1 4.7 %all-to-all-start.3 = ((bf16[32,8,16,128]{3,2,1,0:T(8,128)(2,1)}), bf16[32,8,16,128]{3,2,1,0:T(8,128)(2,1)S(1)}, u32[]{:S(2)}, u32[]{:S(2)}) async-start(bf16[32,8,16,128]{3,2,1,0:T(8,128)(2,1)} %bitcast.30), calls=%async_computation.3 | async-start | bytes 2097152 | tf_op jit(solution)/shard_map/all_to_all | solution.py:313
  189.8 0.9 mul.47.mix
  190.7 23.9 %all-to-all-done.3 = bf16[32,8,16,128]{3,2,1,0:T(8,128)(2,1)S(1)} async-done(((bf16[32,8,16,128]{3,2,1,0:T(8,128)(2,1)}), bf16[32,8,16,128]{3,2,1,0:T(8,128)(2,1)S(1)}, u32[]{:S(2)}, u32[]{:S(2)}) %all-to-all-start.3) | async-done | bytes 1048608 | tf_op jit(solution)/shard_map/all_to_all | solution.py:313
  214.5 0.0 copy-start.1
  214.5 1.0 copy-done.1
  215.5 29.7 %shard_map.144 = bf16[16,64,64,128]{3,2,1,0:T(8,128)(2,1)} custom-call(bf16[8,4,2,4,16,128]{5,4,3,2,1,0:T(8,128)(2,1)} %bitcast.25, bf16[16,64,64,128]{3,2,1,0:T(8,128)(2,1)} %get-tuple-element.12.slope, bf16[256,256]{1,0:T(8,128)(2,1)} %mul.47.mix, bf16[128,512]{1,0:T(8,128)(2,1)} %constant.34.clone.z_adj, bf16[1024,512]{1,0:T(8,128)(2,1)} %constant.37.clone.y_inv, ...), custom_call_target="tpu_custom_call" | custom-call | tf_op jit(solution)/shard_map/pallas_call | solution.py:353
  (1 shorter events, 0.0 us)
Async XLA Ops:
  0.6 66.2 %copy-start.2 = (bf16[64,64]{1,0:T(8,128)(2,1)S(1)}, bf16[64,64]{1,0:T(8,128)(2,1)}, u32[]{:S(2)}) copy-start(bf16[64,64]{1,0:T(8,128)(2,1)} %param.16) | copy-start | bytes 24580
  62.2 29.5 %all-to-all-start.1 = ((bf16[32,8,16,128]{3,2,1,0:T(8,128)(2,1)}), bf16[32,8,16,128]{3,2,1,0:T(8,128)(2,1)S(1)}, u32[]{:S(2)}, u32[]{:S(2)}) async-start(bf16[32,8,16,128]{3,2,1,0:T(8,128)(2,1)} %bitcast.29), calls=%async_computation.1 | async-start | bytes 2097152 | tf_op jit(solution)/shard_map/all_to_all | solution.py:313
  91.7 1.0 copy-start
  185.1 29.5 %all-to-all-start.3 = ((bf16[32,8,16,128]{3,2,1,0:T(8,128)(2,1)}), bf16[32,8,16,128]{3,2,1,0:T(8,128)(2,1)S(1)}, u32[]{:S(2)}, u32[]{:S(2)}) async-start(bf16[32,8,16,128]{3,2,1,0:T(8,128)(2,1)} %bitcast.30), calls=%async_computation.3 | async-start | bytes 2097152 | tf_op jit(solution)/shard_map/all_to_all | solution.py:313
  214.5 1.0 copy-start.1
where the time goes:
time: 247 us; the launch traced here: 245 us
  Pallas kernels  119 us (48%)
  blocking collectives  62 us (25%)
  waiting for transfers between devices  45.9 us (19%)
  starting transfers between devices  9.28 us (4%)
  local copies, waits for them, and re-layouts  7.66 us (3%)
    all_to_all x2, blocking collectives, exchange(): got = lax.all_to_all(flat, axes, split_axis=0, concat_axis=0, tiled=True)  62 us
    pallas_call x1, Pallas kernels, body(): pl.pallas_call(middle_kernel, grid=steps, in_specs=[whole(ins[0]), sliced...  53 us
    all_to_all x2, waiting for transfers between devices, exchange(): got = lax.all_to_all(flat, axes, split_axis=0, concat_axis=0, tiled=True)  45.9 us
    pallas_call x1, Pallas kernels, body(): pl.pallas_call(last_kernel, grid=steps, in_specs=[whole(ins[0]), sliced(s...  29.7 us
    pallas_call x2, Pallas kernels, mode_call(): pl.pallas_call(kernel, grid=(count,), in_specs=[part_spec, w_spec, whole(...  19.3 us
    pallas_call x1, Pallas kernels, body(): pl.pallas_call(first_kernel, grid=steps, in_specs=[sliced(sample.shape)]...  17.5 us
    all_to_all x2, starting transfers between devices, exchange(): got = lax.all_to_all(flat, axes, split_axis=0, concat_axis=0, tiled=True)  9.28 us
  transfers between devices with their start and end apart: 2, of which 2 were waited for; matrix products, arithmetic and copies ran while one was open for 2% of the time, Pallas kernels for 0%

commit v1 on v0

v1 whole, which is shorter than its diff:
```python
import math

import jax
import jax.numpy as jnp
import numpy as np
from jax import lax
from jax.experimental import pallas as pl
from jax.experimental.pallas import tpu as pltpu
from jax.sharding import PartitionSpec as P

BF16 = jnp.bfloat16
F32 = jnp.float32
ROWS = 16
PAIR = 2
YB = 4
VMEM = 67043328
MESH = pl.DeviceIdType.MESH


def waves(length, count, signed, positions=None):
    index = np.arange(count)
    freq = np.where(index < count // 2, index, index - count) if signed else index
    place = np.arange(length if positions is None else positions)
    angle = 2.0 * math.pi * ((place[:, None] * freq[None, :]) % length) / length
    return np.cos(angle), np.sin(angle)


def kron_rows(matrix):
    return np.kron(matrix, np.eye(ROWS))


def const(array):
    return jnp.asarray(np.asarray(array, np.float32), BF16)


def make_tables(nx, ny, nz, fold, packed, mx, my, mz, pencils):
    cx, sx = waves(nx, mx, True)
    cy, sy = waves(ny, my, True, ny // fold)
    cz, sz = waves(nz, mz, False)
    eye_t = np.eye(fold * packed)
    plain = np.concatenate([cz, -sz], 1)
    turned = np.concatenate([-sz, -cz], 1)
    z_fwd = np.concatenate([np.kron(eye_t, plain), np.kron(eye_t, turned)], 1)
    weight = np.where(np.arange(mz) == 0, 1.0, 2.0) / (nx * ny * nz)
    z_inv = np.kron(eye_t, np.concatenate([cz * weight, -sz * weight], 1).T)
    z_adj = np.kron(eye_t, plain.T)
    half = np.eye(mz)
    zero = np.zeros((mz, mz))
    block = np.block([[zero, -half], [half, zero]])
    turn_t = np.kron(eye_t, block)
    turn = np.kron(np.eye(2), turn_t)
    lanes = fold * packed * 2 * mz
    r_fwd = np.zeros((fold, packed, fold, 2 * mz, packed, fold, 2 * mz))
    r_inv = np.zeros((packed, fold, 2 * mz, fold, packed, fold, 2 * mz))
    for b in range(fold):
        for h in range(fold):
            angle = 2.0 * math.pi * ((b * h) % fold) / fold
            c, s = np.cos(angle) * half, np.sin(angle) * half
            for g in range(packed):
                r_fwd[b, g, h, :, g, b, :] = np.block([[c, -s], [s, c]])
                r_inv[g, b, :, b, g, h, :] = np.block([[c, s], [-s, c]])
    r_fwd = r_fwd.reshape(fold * lanes, lanes)
    r_inv = r_inv.reshape(lanes, fold * lanes)
    r_fwd = np.concatenate([r_fwd, r_fwd @ turn_t], 1)
    r_inv = np.concatenate([r_inv, r_inv @ np.kron(np.eye(fold), turn_t)], 1)
    y_fwd = np.concatenate([kron_rows(cy.T), kron_rows(sy.T)], 1)
    y_inv = np.concatenate([kron_rows(cy), -kron_rows(sy)], 1)
    own = nx // pencils
    x_fwd, x_inv = [], []
    for q in range(pencils):
        c, s = cx[q * own : (q + 1) * own], sx[q * own : (q + 1) * own]
        x_fwd.append(np.concatenate([kron_rows(c.T), kron_rows(s.T)], 1))
        x_inv.append(np.concatenate([kron_rows(c), -kron_rows(s)], 1))
    scale = np.tile(np.concatenate([weight, weight]), fold * packed)[None]
    return dict(
        z_fwd=const(z_fwd), z_inv=const(z_inv), z_adj=const(z_adj), turn=const(turn),
        y_fwd=const(y_fwd), y_inv=const(y_inv), r_fwd=const(r_fwd), r_inv=const(r_inv),
        x_fwd=const(np.stack(x_fwd)), x_inv=const(np.stack(x_inv)),
        scale=jnp.asarray(np.asarray(scale, np.float32)),
    )


def mm(a, b):
    return jnp.dot(a, b, preferred_element_type=F32)


def gelu_slope(pre):
    normal_cdf = 0.5 * (1.0 + lax.erf(pre * (1.0 / math.sqrt(2.0))))
    return normal_cdf + pre * jnp.exp(-0.5 * pre * pre) * (1.0 / math.sqrt(2.0 * math.pi))


def rows_of(index):
    return pl.ds(pl.multiple_of(index * ROWS, ROWS), ROWS)


def make_main(dims):
    pd, pp, jxl, jyl, mz, fold, packed, chunks = dims
    n = pd * pp
    nq = jyl // fold
    my = jyl * pp
    lanes = packed * fold * 2 * mz
    hm = fold * mz

    def kernel(
        field, cot, w, w_local, z_fwd, y_fwd, r_fwd, x_fwd, x_inv, turn, r_inv, y_inv, z_inv, scale,
        spread, columns, ucat, gcat,
        fbuf, cbuf, cols, sect, plain_in, turned_in, usend, vsend, bsend,
        urecv, vrecv, grecv, brecv, wbig, tbuf, obuf, xf, xi, mixer,
        fsem, csem, tsem, ssem, rsem, osem, colsem,
    ):
        xl, ny, ch, nz = fbuf.shape
        nyh = ny // fold
        pairs = xl // PAIR
        my_d, my_p = lax.axis_index("dp"), lax.axis_index("pencil")
        me = my_d * pp + my_p
        width = packed * ROWS

        barrier = pltpu.get_barrier_semaphore()

        def greet(i, carry):
            t = lax.rem(me + i, n)
            pl.semaphore_signal(
                barrier, inc=1, device_id=(t // pp, lax.rem(t, pp)), device_id_type=MESH
            )
            return carry

        lax.fori_loop(1, n, greet, 0)

        def piece(ref, g, i):
            return ref.at[pl.ds(i * PAIR, PAIR), :, pl.ds(pl.multiple_of(g * width, width), width), :]

        def load(src, dst, sem, g, i):
            return pltpu.make_async_copy(piece(src, g, i), piece(dst, g, i), sem.at[g, i])

        def start_all(src, dst, sem):
            def one(j, carry):
                load(src, dst, sem, j // pairs, lax.rem(j, pairs)).start()
                return carry

            lax.fori_loop(0, chunks * pairs, one, 0)

        x_tables = [
            pltpu.make_async_copy(x_fwd.at[my_p], xf, tsem.at[0]),
            pltpu.make_async_copy(x_inv.at[my_p], xi, tsem.at[1]),
        ]
        start_all(field, fbuf, fsem)
        for copy in x_tables:
            copy.start()
        start_all(cot, cbuf, csem)
        for copy in x_tables:
            copy.wait()

        def start_sends(source, recv, e, g):
            def one(i, carry):
                t = lax.rem(me + i, n)
                pltpu.make_async_remote_copy(
                    src_ref=source(t), dst_ref=recv.at[g, me],
                    send_sem=ssem.at[e, g], recv_sem=rsem.at[e, g],
                    device_id=(t // pp, lax.rem(t, pp)), device_id_type=MESH,
                ).start()
                return carry

            lax.fori_loop(1, n, one, 0)
            pltpu.make_async_copy(source(me), recv.at[g, me], rsem.at[e, g]).start()

        def wait_recv(recv, e, g):
            pltpu.make_async_copy(recv.at[g], recv.at[g], rsem.at[e, g]).wait()

        def wait_sends(recv, e):
            def one(g, carry):
                sent = recv.at[g, pl.ds(0, n - 1)]
                pltpu.make_async_copy(sent, sent, ssem.at[e, g]).wait()
                return carry

            lax.fori_loop(0, chunks, one, 0)

        def forward_pair(wides, x0):
            plain, turned = [], []
            for wide in wides:
                spectral = mm(wide, z_fwd[...]).astype(BF16)
                plain.append(spectral[:, :lanes])
                turned.append(spectral[:, lanes:])
            stacked = jnp.concatenate([jnp.concatenate(plain, 1), jnp.concatenate(turned, 1)], 0)
            out = mm(y_fwd[...], stacked).astype(BF16)
            for e in range(PAIR):
                sect[x0 + e] = out[:, e * lanes : (e + 1) * lanes]

        def forward_x(send, g):
            tiles = my // fold
            for q0 in range(0, tiles, 2):
                group = range(q0, min(q0 + 2, tiles))
                plain, turned = [], []
                for q in group:
                    rows = jnp.concatenate(
                        [
                            sect[:, (q * fold + b) * ROWS : (q * fold + b + 1) * ROWS, :].reshape(xl * ROWS, lanes)
                            for b in range(fold)
                        ],
                        1,
                    )
                    both = mm(rows, r_fwd[...]).astype(BF16)
                    plain.append(both[:, :lanes])
                    turned.append(both[:, lanes:])
                stacked = jnp.concatenate([jnp.concatenate(plain, 1), jnp.concatenate(turned, 1)], 0)
                got = mm(xf[...], stacked).astype(BF16)
                for e, q in enumerate(group):
                    for d in range(pd):
                        send[g, d * pp + q // nq, q % nq] = got[
                            d * jxl * ROWS : (d + 1) * jxl * ROWS, e * lanes : (e + 1) * lanes
                        ]

        def inverse_x(recv, g):
            tiles = my // fold
            for q0 in range(0, tiles, 2):
                group = range(q0, min(q0 + 2, tiles))
                rows = jnp.concatenate(
                    [
                        jnp.concatenate([recv[g, d * pp + q // nq, q % nq] for d in range(pd)], 0)
                        for q in group
                    ],
                    1,
                )
                size = rows.shape[1]
                turned = mm(rows, turn[:size, :size]).astype(BF16)
                got = mm(xi[...], jnp.concatenate([rows, turned], 0)).astype(BF16)
                for e, q in enumerate(group):
                    wide = mm(got[:, e * lanes : (e + 1) * lanes], r_inv[...]).astype(BF16)
                    for b in range(fold):
                        j = q * fold + b
                        at = slice(j * ROWS, (j + 1) * ROWS)
                        plain_in[:, at, :] = wide[:, b * lanes : (b + 1) * lanes].reshape(xl, ROWS, lanes)
                        turned_in[:, at, :] = wide[
                            :, (fold + b) * lanes : (fold + b + 1) * lanes
                        ].reshape(xl, ROWS, lanes)

        def inverse_y(x0):
            stacked = jnp.concatenate(
                [
                    jnp.concatenate([plain_in[x0 + e] for e in range(PAIR)], 1),
                    jnp.concatenate([turned_in[x0 + e] for e in range(PAIR)], 1),
                ],
                0,
            )
            return mm(y_inv[...], stacked).astype(BF16)

        def places(g):
            for gi in range(packed):
                for h in range(fold):
                    yield pl.ds(h * nyh, nyh), rows_of(g * packed + gi), (gi * fold + h) * nz

        def mix(matrix):
            tiled = jnp.concatenate([matrix] * YB, 1)
            owner = lax.broadcasted_iota(jnp.int32, (1, YB * ch), 1) // ch
            for b in range(YB):
                mixer[b * ch : (b + 1) * ch, :] = jnp.where(owner == b, tiled, 0.0).astype(BF16)

            def one(j, carry):
                x0 = (j // (ny // YB)) * PAIR
                ys = pl.ds(lax.rem(j, ny // YB) * YB, YB)
                wide = jnp.concatenate([fbuf[x0 + e, ys].reshape(YB * ch, nz) for e in range(PAIR)], 1)
                mixed = mm(mixer[...], wide).astype(BF16)
                for e in range(PAIR):
                    fbuf[x0 + e, ys] = mixed[:, e * nz : (e + 1) * nz].reshape(YB, ch, nz)
                return carry

            lax.fori_loop(0, pairs * (ny // YB), one, 0, unroll=2)

        def load_modes(recv, scaled):
            for jx in range(jxl):
                for ql in range(nq):
                    blocks = []
                    for s in range(pd):
                        for c in range(chunks):
                            at = slice(jx * ROWS, (jx + 1) * ROWS)
                            total = recv[c, s * pp, ql, at, :].astype(F32)
                            for q in range(1, pp):
                                total = total + recv[c, s * pp + q, ql, at, :].astype(F32)
                            blocks.append(total)
                    value = jnp.concatenate(blocks, 0)
                    if scaled:
                        value = value * scale[...]
                    flat = value.T
                    for s in range(pd):
                        for b in range(fold):
                            parts = []
                            for ri in range(2):
                                for c in range(chunks):
                                    for gi in range(packed):
                                        top = ((gi * fold + b) * 2 + ri) * mz
                                        left = (s * chunks + c) * ROWS
                                        if packed == 1 and c == 0:
                                            parts.append(flat[top : top + mz, left : left + ch])
                                        elif packed > 1:
                                            parts.append(flat[top : top + mz, left : left + ROWS])
                            low = s * hm + b * mz
                            tbuf[jx * nq + ql, low : low + mz, :] = jnp.concatenate(parts, 1)

        def store_modes(send):
            for jx in range(jxl):
                for ql in range(nq):
                    columns_of = []
                    for s in range(pd):
                        own = obuf[jx * nq + ql, s * hm : (s + 1) * hm, :]
                        if packed == 1:
                            columns_of.append(
                                jnp.concatenate(
                                    [
                                        own[b * mz : (b + 1) * mz, ri * ch : (ri + 1) * ch]
                                        for b in range(fold)
                                        for ri in range(2)
                                    ],
                                    0,
                                )
                            )
                        else:
                            for c in range(chunks):
                                columns_of.append(
                                    jnp.concatenate(
                                        [
                                            own[
                                                b * mz : (b + 1) * mz,
                                                ri * ch + (c * packed + gi) * ROWS : ri * ch + (c * packed + gi + 1) * ROWS,
                                            ]
                                            for gi in range(packed)
                                            for b in range(fold)
                                            for ri in range(2)
                                        ],
                                        0,
                                    )
                                )
                    back = jnp.concatenate(columns_of, 1).T.astype(BF16)
                    for s in range(pd):
                        for c in range(chunks):
                            low = (s * chunks + c) * ROWS
                            send[c, s, ql, jx * ROWS : (jx + 1) * ROWS, :] = back[low : low + ROWS, :]

        def each_mode(apply):
            def one(jq, carry):
                for r in range(hm):
                    own = tbuf[jq, pl.ds(r, pd, stride=hm), :]
                    obuf[jq, pl.ds(r, pd, stride=hm), :] = apply(jq * hm + r, own)
                return carry

            lax.fori_loop(0, jxl * nq, one, 0)

        def first(g, carry):
            def one(i, inner):
                load(field, fbuf, fsem, g, i).wait()
                wides = [
                    jnp.concatenate(
                        [fbuf[i * PAIR + e, ys, cs, :].reshape(nyh * ROWS, nz) for ys, cs, _ in places(g)], 1
                    )
                    for e in range(PAIR)
                ]
                forward_pair(wides, i * PAIR)
                return inner

            lax.fori_loop(0, pairs, one, 0)
            forward_x(usend, g)

            @pl.when(g == 0)
            def _():
                pl.semaphore_wait(barrier, n - 1)

            start_sends(lambda t: usend.at[g, t], urecv, 0, g)
            return carry

        lax.fori_loop(0, chunks, first, 0)

        sign = jnp.where(lax.broadcasted_iota(jnp.int32, (1, 2 * ch), 1) < ch, -1.0, 1.0).astype(F32)

        def prepare(m, carry):
            own = w[m].astype(F32)
            wbig[m, :ch, :] = w[m]
            wbig[m, ch:, :] = (pltpu.roll(own, ch, 1) * sign).astype(BF16)
            return carry

        lax.fori_loop(0, w.shape[0], prepare, 0, unroll=4)
        mix(w_local[...].astype(F32).T)

        def waits(recv, e):
            def one(g, carry):
                wait_recv(recv, e, g)
                return carry

            lax.fori_loop(0, chunks, one, 0)

        waits(urecv, 0)
        load_modes(urecv, False)

        def apply_one(m, own):
            ucat[m] = jnp.concatenate([own, pltpu.roll(own, ch, 1)], 0).astype(BF16)
            return mm(own.astype(BF16), wbig[m])

        each_mode(apply_one)
        store_modes(vsend)

        def send_v(g, carry):
            start_sends(lambda t: vsend.at[g, t // pp], vrecv, 1, g)
            return carry

        lax.fori_loop(0, chunks, send_v, 0)
        wait_sends(urecv, 0)

        def middle(g, carry):
            wait_recv(vrecv, 1, g)
            inverse_x(vrecv, g)

            def one(i, inner):
                load(cot, cbuf, csem, g, i).wait()
                col = inverse_y(i * PAIR)
                wides = []
                for e in range(PAIR):
                    x = i * PAIR + e
                    grid = mm(col[:, e * lanes : (e + 1) * lanes], z_inv[...])
                    pieces = []
                    for ys, cs, left in places(g):
                        pre = grid[:, left : left + nz].reshape(nyh, ROWS, nz) + fbuf[x, ys, cs, :].astype(F32)
                        slope = (cbuf[x, ys, cs, :].astype(F32) * gelu_slope(pre)).astype(BF16)
                        fbuf[x, ys, cs, :] = slope
                        pieces.append(slope.reshape(nyh * ROWS, nz))
                    wides.append(jnp.concatenate(pieces, 1))
                forward_pair(wides, i * PAIR)
                return inner

            lax.fori_loop(0, pairs, one, 0)
            forward_x(usend, g)
            start_sends(lambda t: usend.at[g, t], grecv, 2, g)
            return carry

        lax.fori_loop(0, chunks, middle, 0)

        mix(w_local[...].astype(F32))

        def spread_out(x):
            return pltpu.make_async_copy(fbuf.at[x], spread.at[x], osem.at[x])

        def put(x, carry):
            spread_out(x).start()
            return carry

        lax.fori_loop(0, xl, put, 0)

        waits(grecv, 2)
        load_modes(grecv, True)

        def adjoint_one(m, own):
            own = own.astype(BF16).astype(F32)
            gcat[m] = jnp.concatenate([own, pltpu.roll(own, ch, 1) * -sign], 0).astype(BF16)
            return lax.dot_general(
                own.astype(BF16), wbig[m], (((1,), (1,)), ((), ())), preferred_element_type=F32
            )

        each_mode(adjoint_one)
        store_modes(bsend)

        def send_b(g, carry):
            start_sends(lambda t: bsend.at[g, t // pp], brecv, 3, g)
            return carry

        lax.fori_loop(0, chunks, send_b, 0)

        def cols_out(g, x):
            return pltpu.make_async_copy(cols.at[g, x], columns.at[g, x], colsem.at[g, x])

        def last(g, carry):
            wait_recv(brecv, 3, g)
            inverse_x(brecv, g)

            def one(i, inner):
                col = inverse_y(i * PAIR)
                for e in range(PAIR):
                    cols[g, i * PAIR + e] = col[:, e * lanes : (e + 1) * lanes]
                    cols_out(g, i * PAIR + e).start()
                return inner

            lax.fori_loop(0, pairs, one, 0)
            return carry

        lax.fori_loop(0, chunks, last, 0)
        wait_sends(vrecv, 1)
        wait_sends(grecv, 2)
        wait_sends(brecv, 3)

        def finish(x, carry):
            spread_out(x).wait()
            for g in range(chunks):
                cols_out(g, x).wait()
            return carry

        lax.fori_loop(0, xl, finish, 0)

    return kernel


def make_last(fold, packed, chunks):
    def kernel(spread, columns, z_adj, ucat, gcat, grad, grad_w):
        xs, ny, ch, nz = spread.shape
        nyh = ny // fold
        for x in range(xs):
            for g in range(chunks):
                grid = mm(columns[g, x], z_adj[...])
                for gi in range(packed):
                    for h in range(fold):
                        left = (gi * fold + h) * nz
                        ys = slice(h * nyh, (h + 1) * nyh)
                        cs = slice((g * packed + gi) * ROWS, (g * packed + gi + 1) * ROWS)
                        value = grid[:, left : left + nz].reshape(nyh, ROWS, nz)
                        grad[x, ys, cs, :] = (value + spread[x, ys, cs, :].astype(F32)).astype(BF16)
        for m in range(grad_w.shape[0]):
            grad_w[m] = lax.dot_general(
                ucat[m], gcat[m], (((0,), (0,)), ((), ())), preferred_element_type=F32
            )[:ch]

    return kernel


def whole(array):
    return pl.BlockSpec(array.shape, lambda i, n=len(array.shape): (0,) * n)


def solution(mesh):
    pd, pp = mesh.shape["dp"], mesh.shape["pencil"]

    def body(field, cotangent, w_spec, w_local):
        sample, target = field[0], cotangent[0]
        xl, ny, ch, nz = sample.shape
        jxl, jyl, mz = w_spec.shape[:3]
        mx, my = jxl * pd, jyl * pp
        groups = ch // ROWS
        fold = math.gcd(jyl, groups)
        packed = groups // fold
        chunks = groups // packed
        lanes = groups * 2 * mz
        nq = jyl // fold
        n = pd * pp
        modes = jxl * jyl * mz
        pairs = xl // PAIR
        nyh = ny // fold
        t = make_tables(xl * pp, ny, nz, fold, packed, mx, my, mz, pp)
        weights = w_spec.reshape(modes, ch, 2 * ch)
        hbm = pl.BlockSpec(memory_space=pl.ANY)
        vmem = pl.BlockSpec(memory_space=pltpu.VMEM)
        names = ("z_fwd", "y_fwd", "r_fwd", "x_fwd", "x_inv", "turn", "r_inv", "y_inv", "z_inv", "scale")
        tables = [t[name] for name in names]
        table_specs = [hbm if name in ("x_fwd", "x_inv") else vmem for name in names]
        block = (nq, jxl * ROWS, lanes)
        part = pltpu.VMEM((chunks, n) + block, BF16)
        mode_part = pltpu.VMEM((chunks, pd) + block, BF16)
        section = pltpu.VMEM((xl, my * ROWS, lanes), BF16)
        grid_buf = pltpu.VMEM(sample.shape, BF16)
        by_mode = pltpu.VMEM((jxl * nq, pd * fold * mz, 2 * ch), F32)
        dma = pltpu.SemaphoreType.DMA
        dims = (pd, pp, jxl, jyl, mz, fold, packed, chunks)
        cat = jax.ShapeDtypeStruct((modes, 2 * pd, 2 * ch), BF16)
        spread, columns, ucat, gcat = pl.pallas_call(
            make_main(dims),
            in_specs=[hbm, hbm, vmem, vmem] + table_specs,
            out_specs=[hbm, hbm, vmem, vmem],
            out_shape=[
                jax.ShapeDtypeStruct(sample.shape, BF16),
                jax.ShapeDtypeStruct((chunks, xl, nyh * ROWS, lanes), BF16),
                cat,
                cat,
            ],
            scratch_shapes=[
                grid_buf, grid_buf,
                pltpu.VMEM((chunks, xl, nyh * ROWS, lanes), BF16),
                section, section, section,
                part, mode_part, mode_part,
                part, part, part, part,
                pltpu.VMEM((modes, 2 * ch, 2 * ch), BF16),
                by_mode, by_mode,
                pltpu.VMEM(t["x_fwd"].shape[1:], BF16),
                pltpu.VMEM(t["x_inv"].shape[1:], BF16),
                pltpu.VMEM((YB * ch, YB * ch), BF16),
                dma((chunks, pairs)), dma((chunks, pairs)), dma((2,)),
                dma((4, chunks)), dma((4, chunks)), dma((xl,)), dma((chunks, xl)),
            ],
            compiler_params=pltpu.CompilerParams(
                collective_id=0, has_side_effects=True, vmem_limit_bytes=VMEM
            ),
        )(sample, target, weights, w_local, *tables)

        per = modes // pairs
        grad, grad_w = pl.pallas_call(
            make_last(fold, packed, chunks),
            grid=(pairs,),
            in_specs=[
                pl.BlockSpec((PAIR, ny, ch, nz), lambda i: (i, 0, 0, 0)),
                pl.BlockSpec((chunks, PAIR, nyh * ROWS, lanes), lambda i: (0, i, 0, 0)),
                whole(t["z_adj"]),
                pl.BlockSpec((per, 2 * pd, 2 * ch), lambda i: (i, 0, 0)),
                pl.BlockSpec((per, 2 * pd, 2 * ch), lambda i: (i, 0, 0)),
            ],
            out_specs=[
                pl.BlockSpec((PAIR, ny, ch, nz), lambda i: (i, 0, 0, 0)),
                pl.BlockSpec((per, ch, 2 * ch), lambda i: (i, 0, 0)),
            ],
            out_shape=[
                jax.ShapeDtypeStruct(sample.shape, BF16),
                jax.ShapeDtypeStruct((modes, ch, 2 * ch), F32),
            ],
            compiler_params=pltpu.CompilerParams(
                dimension_semantics=("arbitrary",), vmem_limit_bytes=VMEM
            ),
        )(spread, columns, t["z_adj"], ucat, gcat)
        return grad[None], grad_w.reshape(w_spec.shape)

    grid_spec = P("dp", "pencil", None, None, None)
    return jax.shard_map(
        body,
        mesh=mesh,
        in_specs=(grid_spec, grid_spec, grid_spec, P()),
        out_specs=(grid_spec, grid_spec),
        check_vma=False,
    )
```

time: 247 us -> 214 us (0.87)
  Pallas kernels: 119 us -> 214 us
  blocking collectives: 62 us -> 0 us
  waiting for transfers between devices: 45.9 us -> 0 us
  starting transfers between devices: 9.28 us -> 0 us
  local copies, waits for them, and re-layouts: 7.66 us -> 0 us
    pallas_call x5 -> x2, Pallas kernels: 119 us -> 214 us  [the longest x1 196 us: body(): pl.pallas_call(make_main(dims), in_specs=[hbm, hbm, vmem, vmem] + table_s...]
    all_to_all x2 -> x0, blocking collectives: 62 us -> none  [exchange(): got = lax.all_to_all(flat, axes, split_axis=0, concat_axis=0, tiled=True)]
    all_to_all x2 -> x0, waiting for transfers between devices: 45.9 us -> none  [exchange(): got = lax.all_to_all(flat, axes, split_axis=0, concat_axis=0, tiled=True)]
    all_to_all x2 -> x0, starting transfers between devices: 9.28 us -> none  [exchange(): got = lax.all_to_all(flat, axes, split_axis=0, concat_axis=0, tiled=True)]
    squeeze x2 -> x0, local copies, waits for them, and re-layouts: 3.36 us -> none  [the longest x1 1.69 us: body(): x_fwd = lax.dynamic_index_in_dim(t['x_fwd'], me, 0, keepdims=False)]
  transfers between devices with their start and end apart: 2 -> 0, of which waited for: 2 -> 0; matrix products, arithmetic and copies ran while one was open for 2% -> 0% of each run, Pallas kernels for 0% -> 0%
where the time goes in v1:
time: 214 us
  Pallas kernels  214 us (100%)
    pallas_call x1, Pallas kernels, body(): pl.pallas_call(make_main(dims), in_specs=[hbm, hbm, vmem, vmem] + table_s...  196 us
    pallas_call x1, Pallas kernels, body(): pl.pallas_call(make_last(fold, packed, chunks), grid=(pairs,), in_specs=[...  17.6 us

profile of v1, /device:TPU:0, one launch (start us, length us, event | category | flops | bytes accessed | tf_op | source)
XLA Modules:
  0.0 214.2 jit_solution(8172611392070579784)
XLA Ops:
  0.6 196.0 %shard_map.158 = (bf16[16,64,64,128]{3,2,1,0:T(8,128)(2,1)}, bf16[4,16,256,128]{3,2,1,0:T(8,128)(2,1)}, bf16[128,16,128]{2,1,0:T(8,128)(2,1)}, bf16[128,16,128]{2,1,0:T(8,128)(2,1)}) custom-call(bf16[16,64,64,128]{3,2,1,0:T(8,128)(2,1)} %bitcast.5, bf16[16,64,64,128]{3,2,1,0:T(8,128)(2,1)} %bitcast.6, bf16[128,64,128]{2,1,0:T(8,128)(2,1)} %bitcast.7, ...), custom_call_target="tpu_custom_call" | custom-call | tf_op jit(solution)/shard_map/pallas_call | solution.py:556
  196.7 17.6 %shard_map.159 = (bf16[16,64,64,128]{3,2,1,0:T(8,128)(2,1)}, f32[128,64,128]{2,1,0:T(8,128)}) custom-call(bf16[16,64,64,128]{3,2,1,0:T(8,128)(2,1)} %get-tuple-element.8.spread, bf16[4,16,256,128]{3,2,1,0:T(8,128)(2,1)} %get-tuple-element.9.columns, bf16[128,512]{1,0:T(8,128)(2,1)} %constant.24.clone.z_adj, bf16[128,16,128]{2,1,0:T(8,128)(2,1)} %get-tuple-element.10.ucat, ...), custom_call_target="tpu_custom_call" | custom-call | tf_op jit(solution)/shard_map/pallas_call | solution.py:586

commit v2 on v1

--- a/solution.py
+++ b/solution.py
@@ -13,6 +13,7 @@
 ROWS = 16
 PAIR = 2
 YB = 4
+BATCH = 8
 VMEM = 67043328
 MESH = pl.DeviceIdType.MESH
 
@@ -23,10 +24,6 @@
     place = np.arange(length if positions is None else positions)
     angle = 2.0 * math.pi * ((place[:, None] * freq[None, :]) % length) / length
     return np.cos(angle), np.sin(angle)
-
-
-def kron_rows(matrix):
-    return np.kron(matrix, np.eye(ROWS))
 
 
 def const(array):
@@ -63,19 +60,17 @@
     r_inv = r_inv.reshape(lanes, fold * lanes)
     r_fwd = np.concatenate([r_fwd, r_fwd @ turn_t], 1)
     r_inv = np.concatenate([r_inv, r_inv @ np.kron(np.eye(fold), turn_t)], 1)
-    y_fwd = np.concatenate([kron_rows(cy.T), kron_rows(sy.T)], 1)
-    y_inv = np.concatenate([kron_rows(cy), -kron_rows(sy)], 1)
     own = nx // pencils
-    x_fwd, x_inv = [], []
-    for q in range(pencils):
-        c, s = cx[q * own : (q + 1) * own], sx[q * own : (q + 1) * own]
-        x_fwd.append(np.concatenate([kron_rows(c.T), kron_rows(s.T)], 1))
-        x_inv.append(np.concatenate([kron_rows(c), -kron_rows(s)], 1))
+    cx, sx = cx.reshape(pencils, own, mx), sx.reshape(pencils, own, mx)
+    y_fwd = np.stack([cy.T, sy.T])
+    y_inv = np.stack([cy, -sy])
+    x_fwd = np.stack([cx.transpose(0, 2, 1), sx.transpose(0, 2, 1)], 1)
+    x_inv = np.stack([cx, -sx], 1)
     scale = np.tile(np.concatenate([weight, weight]), fold * packed)[None]
     return dict(
         z_fwd=const(z_fwd), z_inv=const(z_inv), z_adj=const(z_adj), turn=const(turn),
         y_fwd=const(y_fwd), y_inv=const(y_inv), r_fwd=const(r_fwd), r_inv=const(r_inv),
-        x_fwd=const(np.stack(x_fwd)), x_inv=const(np.stack(x_inv)),
+        x_fwd=const(x_fwd), x_inv=const(x_inv),
         scale=jnp.asarray(np.asarray(scale, np.float32)),
     )
 
@@ -87,6 +82,23 @@
 def gelu_slope(pre):
     normal_cdf = 0.5 * (1.0 + lax.erf(pre * (1.0 / math.sqrt(2.0))))
     return normal_cdf + pre * jnp.exp(-0.5 * pre * pre) * (1.0 / math.sqrt(2.0 * math.pi))
+
+
+def expand(small):
+    a, b = small.shape
+    shift = ROWS.bit_length() - 1
+
+    def iota(shape, axis):
+        return lax.broadcasted_iota(jnp.int32, shape, axis)
+
+    def same(left, right):
+        return jnp.where(left == right, 1.0, 0.0).astype(BF16)
+
+    tall, wide, full = (a * ROWS, a), (b, b * ROWS), (a * ROWS, b * ROWS)
+    up = same(iota(tall, 0) >> shift, iota(tall, 1))
+    out = same(iota(wide, 0), iota(wide, 1) >> shift)
+    value = mm(mm(up, small).astype(BF16), out)
+    return jnp.where((iota(full, 0) & (ROWS - 1)) == (iota(full, 1) & (ROWS - 1)), value, 0.0).astype(BF16)
 
 
 def rows_of(index):
@@ -102,15 +114,17 @@
     hm = fold * mz
 
     def kernel(
-        field, cot, w, w_local, z_fwd, y_fwd, r_fwd, x_fwd, x_inv, turn, r_inv, y_inv, z_inv, scale,
+        field, cot, w, w_local, z_fwd, y_small, r_fwd, x_small, x_back, turn, r_inv, y_back, z_inv, scale,
         spread, columns, ucat, gcat,
         fbuf, cbuf, cols, sect, plain_in, turned_in, usend, vsend, bsend,
-        urecv, vrecv, grecv, brecv, wbig, tbuf, obuf, xf, xi, mixer,
-        fsem, csem, tsem, ssem, rsem, osem, colsem,
+        urecv, vrecv, grecv, brecv, wbig, tbuf, obuf, xf, xi, y_fwd, y_inv, mixer, staged, cstage,
+        fsem, csem, ssem, rsem, osem, colsem,
     ):
         xl, ny, ch, nz = fbuf.shape
         nyh = ny // fold
         pairs = xl // PAIR
+        batch = staged.shape[1] // lanes
+        batches = xl // batch
         my_d, my_p = lax.axis_index("dp"), lax.axis_index("pencil")
         me = my_d * pp + my_p
         width = packed * ROWS
@@ -120,7 +134,7 @@
         def greet(i, carry):
             t = lax.rem(me + i, n)
             pl.semaphore_signal(
-                barrier, inc=1, device_id=(t // pp, lax.rem(t, pp)), device_id_type=MESH
+                barrier, inc=1, device_id=(lax.div(t, pp), lax.rem(t, pp)), device_id_type=MESH
             )
             return carry
 
@@ -139,16 +153,12 @@
 
             lax.fori_loop(0, chunks * pairs, one, 0)
 
-        x_tables = [
-            pltpu.make_async_copy(x_fwd.at[my_p], xf, tsem.at[0]),
-            pltpu.make_async_copy(x_inv.at[my_p], xi, tsem.at[1]),
-        ]
         start_all(field, fbuf, fsem)
-        for copy in x_tables:
-            copy.start()
         start_all(cot, cbuf, csem)
-        for copy in x_tables:
-            copy.wait()
+        for table, small in ((xf, x_small.at[my_p]), (xi, x_back.at[my_p]), (y_fwd, y_small), (y_inv, y_back)):
+            half = table.shape[1] // 2
+            for part in range(2):
+                table[:, part * half : (part + 1) * half] = expand(small[part])
 
         def start_sends(source, recv, e, g):
             def one(i, carry):
@@ -156,11 +166,11 @@
                 pltpu.make_async_remote_copy(
                     src_ref=source(t), dst_ref=recv.at[g, me],
                     send_sem=ssem.at[e, g], recv_sem=rsem.at[e, g],
-                    device_id=(t // pp, lax.rem(t, pp)), device_id_type=MESH,
+                    device_id=(lax.div(t, pp), lax.rem(t, pp)), device_id_type=MESH,
                 ).start()
                 return carry
 
-            lax.fori_loop(1, n, one, 0)
+            lax.fori_loop(1, n, one, 0, unroll=8)
             pltpu.make_async_copy(source(me), recv.at[g, me], rsem.at[e, g]).start()
 
         def wait_recv(recv, e, g):
@@ -174,16 +184,17 @@
 
             lax.fori_loop(0, chunks, one, 0)
 
-        def forward_pair(wides, x0):
-            plain, turned = [], []
-            for wide in wides:
-                spectral = mm(wide, z_fwd[...]).astype(BF16)
-                plain.append(spectral[:, :lanes])
-                turned.append(spectral[:, lanes:])
-            stacked = jnp.concatenate([jnp.concatenate(plain, 1), jnp.concatenate(turned, 1)], 0)
-            out = mm(y_fwd[...], stacked).astype(BF16)
-            for e in range(PAIR):
-                sect[x0 + e] = out[:, e * lanes : (e + 1) * lanes]
+        def forward_z(wide, e):
+            spectral = mm(wide, z_fwd[...]).astype(BF16)
+            rows = nyh * ROWS
+            staged[:rows, e * lanes : (e + 1) * lanes] = spectral[:, :lanes]
+            staged[rows:, e * lanes : (e + 1) * lanes] = spectral[:, lanes:]
+
+        def forward_y(x0):
+            for k in range(0, batch, PAIR):
+                out = mm(y_fwd[...], staged[:, k * lanes : (k + PAIR) * lanes]).astype(BF16)
+                for e in range(PAIR):
+                    sect[x0 + k + e] = out[:, e * lanes : (e + 1) * lanes]
 
         def forward_x(send, g):
             tiles = my // fold
@@ -254,16 +265,21 @@
             for b in range(YB):
                 mixer[b * ch : (b + 1) * ch, :] = jnp.where(owner == b, tiled, 0.0).astype(BF16)
 
+            steps = math.gcd(ny // YB, 16)
+            per = ny // YB // steps
+
             def one(j, carry):
-                x0 = (j // (ny // YB)) * PAIR
-                ys = pl.ds(lax.rem(j, ny // YB) * YB, YB)
-                wide = jnp.concatenate([fbuf[x0 + e, ys].reshape(YB * ch, nz) for e in range(PAIR)], 1)
-                mixed = mm(mixer[...], wide).astype(BF16)
-                for e in range(PAIR):
-                    fbuf[x0 + e, ys] = mixed[:, e * nz : (e + 1) * nz].reshape(YB, ch, nz)
+                x0 = (j // per) * PAIR
+                y0 = lax.rem(j, per) * (YB * steps)
+                for u in range(steps):
+                    ys = pl.ds(y0 + u * YB, YB)
+                    wide = jnp.concatenate([fbuf[x0 + e, ys].reshape(YB * ch, nz) for e in range(PAIR)], 1)
+                    mixed = mm(mixer[...], wide).astype(BF16)
+                    for e in range(PAIR):
+                        fbuf[x0 + e, ys] = mixed[:, e * nz : (e + 1) * nz].reshape(YB, ch, nz)
                 return carry
 
-            lax.fori_loop(0, pairs * (ny // YB), one, 0, unroll=2)
+            lax.fori_loop(0, pairs * per, one, 0)
 
         def load_modes(recv, scaled):
             for jx in range(jxl):
@@ -345,17 +361,20 @@
 
         def first(g, carry):
             def one(i, inner):
-                load(field, fbuf, fsem, g, i).wait()
-                wides = [
-                    jnp.concatenate(
-                        [fbuf[i * PAIR + e, ys, cs, :].reshape(nyh * ROWS, nz) for ys, cs, _ in places(g)], 1
+                x0 = i * batch
+                for k in range(batch // PAIR):
+                    load(field, fbuf, fsem, g, i * (batch // PAIR) + k).wait()
+                for e in range(batch):
+                    forward_z(
+                        jnp.concatenate(
+                            [fbuf[x0 + e, ys, cs, :].reshape(nyh * ROWS, nz) for ys, cs, _ in places(g)], 1
+                        ),
+                        e,
                     )
-                    for e in range(PAIR)
-                ]
-                forward_pair(wides, i * PAIR)
+                forward_y(x0)
                 return inner
 
-            lax.fori_loop(0, pairs, one, 0)
+            lax.fori_loop(0, batches, one, 0)
             forward_x(usend, g)
 
             @pl.when(g == 0)
@@ -396,7 +415,7 @@
         store_modes(vsend)
 
         def send_v(g, carry):
-            start_sends(lambda t: vsend.at[g, t // pp], vrecv, 1, g)
+            start_sends(lambda t: vsend.at[g, lax.div(t, pp)], vrecv, 1, g)
             return carry
 
         lax.fori_loop(0, chunks, send_v, 0)
@@ -407,23 +426,24 @@
             inverse_x(vrecv, g)
 
             def one(i, inner):
-                load(cot, cbuf, csem, g, i).wait()
-                col = inverse_y(i * PAIR)
-                wides = []
-                for e in range(PAIR):
-                    x = i * PAIR + e
-                    grid = mm(col[:, e * lanes : (e + 1) * lanes], z_inv[...])
+                x0 = i * batch
+                for k in range(batch // PAIR):
+                    load(cot, cbuf, csem, g, i * (batch // PAIR) + k).wait()
+                for k in range(0, batch, PAIR):
+                    cstage[:, k * lanes : (k + PAIR) * lanes] = inverse_y(x0 + k)
+                for e in range(batch):
+                    grid = mm(cstage[:, e * lanes : (e + 1) * lanes], z_inv[...])
                     pieces = []
                     for ys, cs, left in places(g):
-                        pre = grid[:, left : left + nz].reshape(nyh, ROWS, nz) + fbuf[x, ys, cs, :].astype(F32)
-                        slope = (cbuf[x, ys, cs, :].astype(F32) * gelu_slope(pre)).astype(BF16)
-                        fbuf[x, ys, cs, :] = slope
+                        pre = grid[:, left : left + nz].reshape(nyh, ROWS, nz) + fbuf[x0 + e, ys, cs, :].astype(F32)
+                        slope = (cbuf[x0 + e, ys, cs, :].astype(F32) * gelu_slope(pre)).astype(BF16)
+                        fbuf[x0 + e, ys, cs, :] = slope
                         pieces.append(slope.reshape(nyh * ROWS, nz))
-                    wides.append(jnp.concatenate(pieces, 1))
-                forward_pair(wides, i * PAIR)
+                    forward_z(jnp.concatenate(pieces, 1), e)
+                forward_y(x0)
                 return inner
 
-            lax.fori_loop(0, pairs, one, 0)
+            lax.fori_loop(0, batches, one, 0)
             forward_x(usend, g)
             start_sends(lambda t: usend.at[g, t], grecv, 2, g)
             return carry
@@ -455,7 +475,7 @@
         store_modes(bsend)
 
         def send_b(g, carry):
-            start_sends(lambda t: bsend.at[g, t // pp], brecv, 3, g)
+            start_sends(lambda t: bsend.at[g, lax.div(t, pp)], brecv, 3, g)
             return carry
 
         lax.fori_loop(0, chunks, send_b, 0)
@@ -468,13 +488,20 @@
             inverse_x(brecv, g)
 
             def one(i, inner):
-                col = inverse_y(i * PAIR)
-                for e in range(PAIR):
-                    cols[g, i * PAIR + e] = col[:, e * lanes : (e + 1) * lanes]
-                    cols_out(g, i * PAIR + e).start()
+                for k in range(0, batch, PAIR):
+                    x0 = i * batch + k
+                    col = inverse_y(x0)
+                    for e in range(PAIR):
+                        cols[g, x0 + e] = col[:, e * lanes : (e + 1) * lanes]
                 return inner
 
-            lax.fori_loop(0, pairs, one, 0)
+            lax.fori_loop(0, batches, one, 0)
+
+            def out(x, inner):
+                cols_out(g, x).start()
+                return inner
+
+            lax.fori_loop(0, xl, out, 0)
             return carry
 
         lax.fori_loop(0, chunks, last, 0)
@@ -543,7 +570,8 @@
         vmem = pl.BlockSpec(memory_space=pltpu.VMEM)
         names = ("z_fwd", "y_fwd", "r_fwd", "x_fwd", "x_inv", "turn", "r_inv", "y_inv", "z_inv", "scale")
         tables = [t[name] for name in names]
-        table_specs = [hbm if name in ("x_fwd", "x_inv") else vmem for name in names]
+        table_specs = [vmem] * len(names)
+        batch = math.gcd(xl, BATCH)
         block = (nq, jxl * ROWS, lanes)
         part = pltpu.VMEM((chunks, n) + block, BF16)
         mode_part = pltpu.VMEM((chunks, pd) + block, BF16)
@@ -571,10 +599,14 @@
                 part, part, part, part,
                 pltpu.VMEM((modes, 2 * ch, 2 * ch), BF16),
                 by_mode, by_mode,
-                pltpu.VMEM(t["x_fwd"].shape[1:], BF16),
-                pltpu.VMEM(t["x_inv"].shape[1:], BF16),
+                pltpu.VMEM((mx * ROWS, 2 * xl * ROWS), BF16),
+                pltpu.VMEM((xl * ROWS, 2 * mx * ROWS), BF16),
+                pltpu.VMEM((my * ROWS, 2 * nyh * ROWS), BF16),
+                pltpu.VMEM((nyh * ROWS, 2 * my * ROWS), BF16),
                 pltpu.VMEM((YB * ch, YB * ch), BF16),
-                dma((chunks, pairs)), dma((chunks, pairs)), dma((2,)),
+                pltpu.VMEM((2 * nyh * ROWS, batch * lanes), BF16),
+                pltpu.VMEM((nyh * ROWS, batch * lanes), BF16),
+                dma((chunks, pairs)), dma((chunks, pairs)),
                 dma((4, chunks)), dma((4, chunks)), dma((xl,)), dma((chunks, xl)),
             ],
             compiler_params=pltpu.CompilerParams(

time: 214 us -> 142 us (0.66)
  Pallas kernels: 214 us -> 141 us
    pallas_call x1, Pallas kernels: 196 us -> 123 us  [body(): pl.pallas_call(make_main(dims), in_specs=[hbm, hbm, vmem, vmem] + table_s...]
where the time goes in v2:
time: 142 us; the launch traced here: 141 us
  Pallas kernels  141 us (99%)
    pallas_call x1, Pallas kernels, body(): pl.pallas_call(make_main(dims), in_specs=[hbm, hbm, vmem, vmem] + table_s...  123 us
    pallas_call x1, Pallas kernels, body(): pl.pallas_call(make_last(fold, packed, chunks), grid=(pairs,), in_specs=[...  17.6 us

profile of v2, /device:TPU:0, one launch (start us, length us, event | category | flops | bytes accessed | tf_op | source)
XLA Modules:
  0.0 141.4 jit_solution(1634659211349264966)
XLA Ops:
  0.6 123.2 %shard_map.158 = (bf16[16,64,64,128]{3,2,1,0:T(8,128)(2,1)}, bf16[4,16,256,128]{3,2,1,0:T(8,128)(2,1)}, bf16[128,16,128]{2,1,0:T(8,128)(2,1)}, bf16[128,16,128]{2,1,0:T(8,128)(2,1)}) custom-call(bf16[16,64,64,128]{3,2,1,0:T(8,128)(2,1)} %bitcast.5, bf16[16,64,64,128]{3,2,1,0:T(8,128)(2,1)} %bitcast.6, bf16[128,64,128]{2,1,0:T(8,128)(2,1)} %bitcast.7, ...), custom_call_target="tpu_custom_call" | custom-call | tf_op jit(solution)/shard_map/pallas_call | solution.py:584
  123.8 17.6 %shard_map.159 = (bf16[16,64,64,128]{3,2,1,0:T(8,128)(2,1)}, f32[128,64,128]{2,1,0:T(8,128)}) custom-call(bf16[16,64,64,128]{3,2,1,0:T(8,128)(2,1)} %get-tuple-element.8.spread, bf16[4,16,256,128]{3,2,1,0:T(8,128)(2,1)} %get-tuple-element.9.columns, bf16[128,512]{1,0:T(8,128)(2,1)} %constant.24.clone.z_adj, bf16[128,16,128]{2,1,0:T(8,128)(2,1)} %get-tuple-element.10.ucat, ...), custom_call_target="tpu_custom_call" | custom-call | tf_op jit(solution)/shard_map/pallas_call | solution.py:618

commit v3 on v2

--- a/solution.py
+++ b/solution.py
@@ -14,6 +14,7 @@
 PAIR = 2
 YB = 4
 BATCH = 8
+LAST = 4
 VMEM = 67043328
 MESH = pl.DeviceIdType.MESH
 
@@ -39,7 +40,7 @@
     turned = np.concatenate([-sz, -cz], 1)
     z_fwd = np.concatenate([np.kron(eye_t, plain), np.kron(eye_t, turned)], 1)
     weight = np.where(np.arange(mz) == 0, 1.0, 2.0) / (nx * ny * nz)
-    z_inv = np.kron(eye_t, np.concatenate([cz * weight, -sz * weight], 1).T)
+    z_inv = np.kron(eye_t, np.concatenate([cz * weight, -sz * weight], 1).T) * math.sqrt(0.5)
     z_adj = np.kron(eye_t, plain.T)
     half = np.eye(mz)
     zero = np.zeros((mz, mz))
@@ -66,7 +67,7 @@
     y_inv = np.stack([cy, -sy])
     x_fwd = np.stack([cx.transpose(0, 2, 1), sx.transpose(0, 2, 1)], 1)
     x_inv = np.stack([cx, -sx], 1)
-    scale = np.tile(np.concatenate([weight, weight]), fold * packed)[None]
+    scale = 0.5 * np.tile(np.concatenate([weight, weight]), fold * packed)[None]
     return dict(
         z_fwd=const(z_fwd), z_inv=const(z_inv), z_adj=const(z_adj), turn=const(turn),
         y_fwd=const(y_fwd), y_inv=const(y_inv), r_fwd=const(r_fwd), r_inv=const(r_inv),
@@ -79,9 +80,9 @@
     return jnp.dot(a, b, preferred_element_type=F32)
 
 
-def gelu_slope(pre):
-    normal_cdf = 0.5 * (1.0 + lax.erf(pre * (1.0 / math.sqrt(2.0))))
-    return normal_cdf + pre * jnp.exp(-0.5 * pre * pre) * (1.0 / math.sqrt(2.0 * math.pi))
+def twice_gelu_slope(q):
+    bell = jnp.exp2((q * q) * (-1.0 / math.log(2.0)))
+    return (1.0 + lax.erf(q)) + q * bell * (2.0 / math.sqrt(math.pi))
 
 
 def expand(small):
@@ -118,7 +119,7 @@
         spread, columns, ucat, gcat,
         fbuf, cbuf, cols, sect, plain_in, turned_in, usend, vsend, bsend,
         urecv, vrecv, grecv, brecv, wbig, tbuf, obuf, xf, xi, y_fwd, y_inv, mixer, staged, cstage,
-        fsem, csem, ssem, rsem, osem, colsem,
+        fsem, csem, ssem, rsem, csend, crecv, relayed, osem, colsem,
     ):
         xl, ny, ch, nz = fbuf.shape
         nyh = ny // fold
@@ -155,10 +156,14 @@
 
         start_all(field, fbuf, fsem)
         start_all(cot, cbuf, csem)
-        for table, small in ((xf, x_small.at[my_p]), (xi, x_back.at[my_p]), (y_fwd, y_small), (y_inv, y_back)):
+
+        def fill(table, small):
             half = table.shape[1] // 2
             for part in range(2):
                 table[:, part * half : (part + 1) * half] = expand(small[part])
+
+        fill(y_fwd, y_small)
+        fill(xf, x_small.at[my_p])
 
         def start_sends(source, recv, e, g):
             def one(i, carry):
@@ -180,6 +185,76 @@
             def one(g, carry):
                 sent = recv.at[g, pl.ds(0, n - 1)]
                 pltpu.make_async_copy(sent, sent, ssem.at[e, g]).wait()
+                return carry
+
+            lax.fori_loop(0, chunks, one, 0)
+
+        half = pp // 2
+        side = lax.div(my_p, half)
+        reach = half + 1
+        lowest = side * (half - 1)
+
+        def start_cast(source, recv, e, g):
+            place = my_p * pd + my_d
+            own = my_d * reach + my_p - lowest
+
+            def one(i, carry):
+                t = lax.rem(own + i, pd * reach)
+                s = lax.div(t, reach)
+                pltpu.make_async_remote_copy(
+                    src_ref=source.at[g, s], dst_ref=recv.at[g, place],
+                    send_sem=csend.at[e, g], recv_sem=crecv.at[e, side, g],
+                    device_id=(s, lowest + lax.rem(t, reach)), device_id_type=MESH,
+                ).start()
+                return carry
+
+            lax.fori_loop(1, pd * reach, one, 0, unroll=8)
+            pltpu.make_async_copy(source.at[g, my_d], recv.at[g, place], crecv.at[e, side, g]).start()
+
+        def part_of(recv, g, which):
+            return recv.at[g, pl.ds(which * half * pd, half * pd)]
+
+        def wait_part(recv, e, g, which):
+            part = part_of(recv, g, which)
+            pltpu.make_async_copy(part, part, crecv.at[e, which, g]).wait()
+
+        def pass_on(recv, e, g, which, r):
+            part = part_of(recv, g, which)
+            target = half + 1 + r if which == 0 else r
+            return pltpu.make_async_remote_copy(
+                src_ref=part, dst_ref=part,
+                send_sem=relayed.at[e, g, r], recv_sem=crecv.at[e, which, g],
+                device_id=(my_d, target), device_id_type=MESH,
+            )
+
+        def relay(recv, e, g):
+            for which in range(2):
+
+                @pl.when(my_p == half - which)
+                def _():
+                    wait_part(recv, e, g, which)
+                    for r in range(half - 1):
+                        pass_on(recv, e, g, which, r).start()
+
+        def wait_cast(recv, e, g):
+            for which in range(2):
+
+                @pl.when(my_p != half - which)
+                def _():
+                    wait_part(recv, e, g, which)
+
+        def end_cast(recv, e):
+            def one(g, carry):
+                sent = recv.at[g, pl.ds(0, pd * reach - 1)]
+                pltpu.make_async_copy(sent, sent, csend.at[e, g]).wait()
+                for which in range(2):
+
+                    @pl.when(my_p == half - which)
+                    def _():
+                        part = part_of(recv, g, which)
+                        for r in range(half - 1):
+                            pltpu.make_async_copy(part, part, relayed.at[e, g, r]).wait()
+
                 return carry
 
             lax.fori_loop(0, chunks, one, 0)
@@ -226,7 +301,7 @@
                 group = range(q0, min(q0 + 2, tiles))
                 rows = jnp.concatenate(
                     [
-                        jnp.concatenate([recv[g, d * pp + q // nq, q % nq] for d in range(pd)], 0)
+                        jnp.concatenate([recv[g, (q // nq) * pd + d, q % nq] for d in range(pd)], 0)
                         for q in group
                     ],
                     1,
@@ -259,7 +334,7 @@
                 for h in range(fold):
                     yield pl.ds(h * nyh, nyh), rows_of(g * packed + gi), (gi * fold + h) * nz
 
-        def mix(matrix):
+        def mix(matrix, factor):
             tiled = jnp.concatenate([matrix] * YB, 1)
             owner = lax.broadcasted_iota(jnp.int32, (1, YB * ch), 1) // ch
             for b in range(YB):
@@ -274,7 +349,7 @@
                 for u in range(steps):
                     ys = pl.ds(y0 + u * YB, YB)
                     wide = jnp.concatenate([fbuf[x0 + e, ys].reshape(YB * ch, nz) for e in range(PAIR)], 1)
-                    mixed = mm(mixer[...], wide).astype(BF16)
+                    mixed = (mm(mixer[...], wide) * factor).astype(BF16)
                     for e in range(PAIR):
                         fbuf[x0 + e, ys] = mixed[:, e * nz : (e + 1) * nz].reshape(YB, ch, nz)
                 return carry
@@ -395,7 +470,9 @@
             return carry
 
         lax.fori_loop(0, w.shape[0], prepare, 0, unroll=4)
-        mix(w_local[...].astype(F32).T)
+        fill(y_inv, y_back)
+        fill(xi, x_back.at[my_p])
+        mix(w_local[...].astype(F32).T, math.sqrt(0.5))
 
         def waits(recv, e):
             def one(g, carry):
@@ -415,15 +492,24 @@
         store_modes(vsend)
 
         def send_v(g, carry):
-            start_sends(lambda t: vsend.at[g, lax.div(t, pp)], vrecv, 1, g)
+            start_cast(vsend, vrecv, 0, g)
             return carry
 
         lax.fori_loop(0, chunks, send_v, 0)
         wait_sends(urecv, 0)
 
         def middle(g, carry):
-            wait_recv(vrecv, 1, g)
+            @pl.when(g == 0)
+            def _():
+                relay(vrecv, 0, g)
+
+            wait_cast(vrecv, 0, g)
             inverse_x(vrecv, g)
+
+            @pl.when(g < chunks - 1)
+            def _():
+                relay(vrecv, 0, g + 1)
+
 
             def one(i, inner):
                 x0 = i * batch
@@ -435,8 +521,8 @@
                     grid = mm(cstage[:, e * lanes : (e + 1) * lanes], z_inv[...])
                     pieces = []
                     for ys, cs, left in places(g):
-                        pre = grid[:, left : left + nz].reshape(nyh, ROWS, nz) + fbuf[x0 + e, ys, cs, :].astype(F32)
-                        slope = (cbuf[x0 + e, ys, cs, :].astype(F32) * gelu_slope(pre)).astype(BF16)
+                        q = grid[:, left : left + nz].reshape(nyh, ROWS, nz) + fbuf[x0 + e, ys, cs, :].astype(F32)
+                        slope = (cbuf[x0 + e, ys, cs, :].astype(F32) * twice_gelu_slope(q)).astype(BF16)
                         fbuf[x0 + e, ys, cs, :] = slope
                         pieces.append(slope.reshape(nyh * ROWS, nz))
                     forward_z(jnp.concatenate(pieces, 1), e)
@@ -445,12 +531,12 @@
 
             lax.fori_loop(0, batches, one, 0)
             forward_x(usend, g)
-            start_sends(lambda t: usend.at[g, t], grecv, 2, g)
+            start_sends(lambda t: usend.at[g, t], grecv, 1, g)
             return carry
 
         lax.fori_loop(0, chunks, middle, 0)
 
-        mix(w_local[...].astype(F32))
+        mix(w_local[...].astype(F32) * 0.5, 1.0)
 
         def spread_out(x):
             return pltpu.make_async_copy(fbuf.at[x], spread.at[x], osem.at[x])
@@ -461,7 +547,7 @@
 
         lax.fori_loop(0, xl, put, 0)
 
-        waits(grecv, 2)
+        waits(grecv, 1)
         load_modes(grecv, True)
 
         def adjoint_one(m, own):
@@ -475,7 +561,7 @@
         store_modes(bsend)
 
         def send_b(g, carry):
-            start_sends(lambda t: bsend.at[g, lax.div(t, pp)], brecv, 3, g)
+            start_cast(bsend, brecv, 1, g)
             return carry
 
         lax.fori_loop(0, chunks, send_b, 0)
@@ -484,7 +570,8 @@
             return pltpu.make_async_copy(cols.at[g, x], columns.at[g, x], colsem.at[g, x])
 
         def last(g, carry):
-            wait_recv(brecv, 3, g)
+            relay(brecv, 1, g)
+            wait_cast(brecv, 1, g)
             inverse_x(brecv, g)
 
             def one(i, inner):
@@ -505,9 +592,9 @@
             return carry
 
         lax.fori_loop(0, chunks, last, 0)
-        wait_sends(vrecv, 1)
-        wait_sends(grecv, 2)
-        wait_sends(brecv, 3)
+        end_cast(vrecv, 0)
+        wait_sends(grecv, 1)
+        end_cast(brecv, 1)
 
         def finish(x, carry):
             spread_out(x).wait()
@@ -607,26 +694,29 @@
                 pltpu.VMEM((2 * nyh * ROWS, batch * lanes), BF16),
                 pltpu.VMEM((nyh * ROWS, batch * lanes), BF16),
                 dma((chunks, pairs)), dma((chunks, pairs)),
-                dma((4, chunks)), dma((4, chunks)), dma((xl,)), dma((chunks, xl)),
+                dma((2, chunks)), dma((2, chunks)),
+                dma((2, chunks)), dma((2, 2, chunks)), dma((2, chunks, max(pp // 2 - 1, 1))), dma((xl,)), dma((chunks, xl)),
             ],
             compiler_params=pltpu.CompilerParams(
                 collective_id=0, has_side_effects=True, vmem_limit_bytes=VMEM
             ),
         )(sample, target, weights, w_local, *tables)
 
-        per = modes // pairs
+        rows = math.gcd(xl, LAST)
+        steps = xl // rows
+        per = modes // steps
         grad, grad_w = pl.pallas_call(
             make_last(fold, packed, chunks),
-            grid=(pairs,),
+            grid=(steps,),
             in_specs=[
-                pl.BlockSpec((PAIR, ny, ch, nz), lambda i: (i, 0, 0, 0)),
-                pl.BlockSpec((chunks, PAIR, nyh * ROWS, lanes), lambda i: (0, i, 0, 0)),
+                pl.BlockSpec((rows, ny, ch, nz), lambda i: (i, 0, 0, 0)),
+                pl.BlockSpec((chunks, rows, nyh * ROWS, lanes), lambda i: (0, i, 0, 0)),
                 whole(t["z_adj"]),
                 pl.BlockSpec((per, 2 * pd, 2 * ch), lambda i: (i, 0, 0)),
                 pl.BlockSpec((per, 2 * pd, 2 * ch), lambda i: (i, 0, 0)),
             ],
             out_specs=[
-                pl.BlockSpec((PAIR, ny, ch, nz), lambda i: (i, 0, 0, 0)),
+                pl.BlockSpec((rows, ny, ch, nz), lambda i: (i, 0, 0, 0)),
                 pl.BlockSpec((per, ch, 2 * ch), lambda i: (i, 0, 0)),
             ],
             out_shape=[

time: 142 us -> 131 us (0.923)
  Pallas kernels: 141 us -> 130 us
    pallas_call x1, Pallas kernels: 123 us -> 115 us  [body(): pl.pallas_call(make_main(dims), in_specs=[hbm, hbm, vmem, vmem] + table_s...]
    pallas_call x1, Pallas kernels: 17.6 us -> 15.1 us  [body(): pl.pallas_call(make_last(fold, packed, chunks), grid=(steps,), in_specs=[...]
where the time goes in v3:
time: 131 us
  Pallas kernels  130 us (99%)
    pallas_call x1, Pallas kernels, body(): pl.pallas_call(make_main(dims), in_specs=[hbm, hbm, vmem, vmem] + table_s...  115 us
    pallas_call x1, Pallas kernels, body(): pl.pallas_call(make_last(fold, packed, chunks), grid=(steps,), in_specs=[...  15.1 us

profile of v3, /device:TPU:0, one launch (start us, length us, event | category | flops | bytes accessed | tf_op | source)
XLA Modules:
  0.0 130.6 jit_solution(6586994168105012699)
XLA Ops:
  0.6 114.8 %shard_map.158 = (bf16[16,64,64,128]{3,2,1,0:T(8,128)(2,1)}, bf16[4,16,256,128]{3,2,1,0:T(8,128)(2,1)}, bf16[128,16,128]{2,1,0:T(8,128)(2,1)}, bf16[128,16,128]{2,1,0:T(8,128)(2,1)}) custom-call(bf16[16,64,64,128]{3,2,1,0:T(8,128)(2,1)} %bitcast.5, bf16[16,64,64,128]{3,2,1,0:T(8,128)(2,1)} %bitcast.6, bf16[128,64,128]{2,1,0:T(8,128)(2,1)} %bitcast.7, ...), custom_call_target="tpu_custom_call" | custom-call | tf_op jit(solution)/shard_map/pallas_call | solution.py:671
  115.5 15.1 %shard_map.159 = (bf16[16,64,64,128]{3,2,1,0:T(8,128)(2,1)}, f32[128,64,128]{2,1,0:T(8,128)}) custom-call(bf16[16,64,64,128]{3,2,1,0:T(8,128)(2,1)} %get-tuple-element.8.spread, bf16[4,16,256,128]{3,2,1,0:T(8,128)(2,1)} %get-tuple-element.9.columns, bf16[128,512]{1,0:T(8,128)(2,1)} %constant.24.clone.z_adj, bf16[128,16,128]{2,1,0:T(8,128)(2,1)} %get-tuple-element.10.ucat, ...), custom_call_target="tpu_custom_call" | custom-call | tf_op jit(solution)/shard_map/pallas_call | solution.py:708

commit v4 on v3

--- a/solution.py
+++ b/solution.py
@@ -192,23 +192,30 @@
         half = pp // 2
         side = lax.div(my_p, half)
         reach = half + 1
-        lowest = side * (half - 1)
 
         def start_cast(source, recv, e, g):
             place = my_p * pd + my_d
-            own = my_d * reach + my_p - lowest
-
-            def one(i, carry):
-                t = lax.rem(own + i, pd * reach)
-                s = lax.div(t, reach)
+
+            def send(s, q):
                 pltpu.make_async_remote_copy(
                     src_ref=source.at[g, s], dst_ref=recv.at[g, place],
                     send_sem=csend.at[e, g], recv_sem=crecv.at[e, side, g],
-                    device_id=(s, lowest + lax.rem(t, reach)), device_id_type=MESH,
+                    device_id=(s, q), device_id_type=MESH,
                 ).start()
-                return carry
-
-            lax.fori_loop(1, pd * reach, one, 0, unroll=8)
+
+            for step in range(reach):
+                q = half - side + step * (2 * side - 1)
+
+                def one(i, carry):
+                    send(lax.rem(my_d + i, pd), q)
+                    return carry
+
+                lax.fori_loop(1, pd, one, 0, unroll=7)
+
+                @pl.when(q != my_p)
+                def _():
+                    send(my_d, q)
+
             pltpu.make_async_copy(source.at[g, my_d], recv.at[g, place], crecv.at[e, side, g]).start()
 
         def part_of(recv, g, which):

time: 131 us -> 130 us (level)
  no operation moved by 1% of the time
where the time goes in v4:
time: 130 us
  Pallas kernels  129 us (99%)
    pallas_call x1, Pallas kernels, body(): pl.pallas_call(make_main(dims), in_specs=[hbm, hbm, vmem, vmem] + table_s...  114 us
    pallas_call x1, Pallas kernels, body(): pl.pallas_call(make_last(fold, packed, chunks), grid=(steps,), in_specs=[...  15.1 us

profile of v4, /device:TPU:0, one launch (start us, length us, event | category | flops | bytes accessed | tf_op | source)
XLA Modules:
  0.0 129.7 jit_solution(2682191162384601799)
XLA Ops:
  0.6 113.9 %shard_map.158 = (bf16[16,64,64,128]{3,2,1,0:T(8,128)(2,1)}, bf16[4,16,256,128]{3,2,1,0:T(8,128)(2,1)}, bf16[128,16,128]{2,1,0:T(8,128)(2,1)}, bf16[128,16,128]{2,1,0:T(8,128)(2,1)}) custom-call(bf16[16,64,64,128]{3,2,1,0:T(8,128)(2,1)} %bitcast.5, bf16[16,64,64,128]{3,2,1,0:T(8,128)(2,1)} %bitcast.6, bf16[128,64,128]{2,1,0:T(8,128)(2,1)} %bitcast.7, ...), custom_call_target="tpu_custom_call" | custom-call | tf_op jit(solution)/shard_map/pallas_call | solution.py:678
  114.5 15.1 %shard_map.159 = (bf16[16,64,64,128]{3,2,1,0:T(8,128)(2,1)}, f32[128,64,128]{2,1,0:T(8,128)}) custom-call(bf16[16,64,64,128]{3,2,1,0:T(8,128)(2,1)} %get-tuple-element.8.spread, bf16[4,16,256,128]{3,2,1,0:T(8,128)(2,1)} %get-tuple-element.9.columns, bf16[128,512]{1,0:T(8,128)(2,1)} %constant.24.clone.z_adj, bf16[128,16,128]{2,1,0:T(8,128)(2,1)} %get-tuple-element.10.ucat, ...), custom_call_target="tpu_custom_call" | custom-call | tf_op jit(solution)/shard_map/pallas_call | solution.py:715
